TPU v7x, 32 devices: a whole 2x2x4 slice. The times are simulated.
32 devices in a mesh: grp: 2 (over y), theta: 8 (over z, x), phi: 2 (over core).
Axes of the slice: x: 2, y: 2, z: 4, core: 2. Of those that a mesh axis runs over, the one named last changes fastest.
Arguments:
- maps: bfloat16 [8, 4096, 4096], P('grp', 'theta', 'phi'), parts along dimension 0, may hold values from -6 to 6
- deltas: bfloat16 [4096, 4, 4096], P('phi', None, 'theta'), may hold values from -1 to 1
- spin_rows: bfloat16 [4096, 2, 4], P('phi'), may hold values from -1 to 1
- ell_index: int32 [4], replicated, may hold values from 1024 to 2047
- owner_map: int32 [4096], replicated, may hold values from 0 to 4095, each once
- prior: float32 [4], replicated, may hold values from 0.3 to 3
Outputs:
- gradient: float32 [8, 2, 4096], P('grp', None, ('theta', 'phi')), parts along dimension 0
There are 2 independent parts, one for each index of `grp`. A program takes and returns all parts, laid end to end along the dimension named above; an argument that names none is the same for every part. Nothing has to cross between parts.
Inputs may be any that keep to these rules, and one draw needn't show every extreme that they name: `ell_index`: every selected degree is at least 1024; tables may repeat a degree. A permutation of the Fourier indices; slot s of deltas and of the output belongs to the frequency owner_map[s].
All inputs are finite; a program needn't handle non-finite values.
Results may differ from a plain program's by a relative error of at most 0.0003.
Values may be sent and summed in bfloat16 or wider, within the bound.
A program may use at most 256 MiB of HBM per device.

v0:
```python
import math
import jax
import jax.numpy as jnp
from jax import lax
from jax.sharding import PartitionSpec as P


def exact_einsum(form, table, operand):
    return jnp.einsum(form, table, operand, precision=lax.Precision.HIGHEST)


def angle_tables(row_count, start, count, modulus):
    freq_rows = jnp.arange(row_count, dtype=jnp.int32)
    sample_cols = start + jnp.arange(count, dtype=jnp.int32)
    angles = (
        2.0
        * math.pi
        / modulus
        * jnp.mod(freq_rows[:, None] * sample_cols[None, :], modulus).astype(jnp.float32)
    )
    return (jnp.cos(angles), jnp.sin(angles))


def row_transform(real_part, imag_part, outer_len, inner_len):
    row_count = real_part.shape[0]
    length = outer_len * inner_len
    cos_a, sin_a = angle_tables(outer_len, 0, outer_len, outer_len)
    real_blocks = real_part.reshape(row_count, outer_len, inner_len)
    section_real = exact_einsum("ka,rab->rkb", cos_a, real_blocks)
    section_imag = -exact_einsum("ka,rab->rkb", sin_a, real_blocks)
    if imag_part is not None:
        imag_blocks = imag_part.reshape(row_count, outer_len, inner_len)
        section_real = section_real + exact_einsum("ka,rab->rkb", sin_a, imag_blocks)
        section_imag = section_imag + exact_einsum("ka,rab->rkb", cos_a, imag_blocks)
    cos_t, sin_t = angle_tables(outer_len, 0, inner_len, length)
    turned_real = section_real * cos_t + section_imag * sin_t
    turned_imag = section_imag * cos_t - section_real * sin_t
    cos_b, sin_b = angle_tables(inner_len, 0, inner_len, inner_len)
    out_real = exact_einsum("qb,rkb->rqk", cos_b, turned_real) + exact_einsum(
        "qb,rkb->rqk", sin_b, turned_imag
    )
    out_imag = exact_einsum("qb,rkb->rqk", cos_b, turned_imag) - exact_einsum(
        "qb,rkb->rqk", sin_b, turned_real
    )
    return (out_real.reshape(row_count, length), out_imag.reshape(row_count, length))


def column_transform(real_part, imag_part, outer_len, inner_len, start):
    fields = real_part.shape[0]
    count = real_part.shape[2]
    slots = real_part.shape[3]
    length = outer_len * inner_len
    cos_a, sin_a = angle_tables(outer_len, 0, outer_len, outer_len)
    section_real = exact_einsum("ka,fabm->fkbm", cos_a, real_part) + exact_einsum(
        "ka,fabm->fkbm", sin_a, imag_part
    )
    section_imag = exact_einsum("ka,fabm->fkbm", cos_a, imag_part) - exact_einsum(
        "ka,fabm->fkbm", sin_a, real_part
    )
    cos_t, sin_t = angle_tables(outer_len, start, count, length)
    cos_t = cos_t[:, :, None]
    sin_t = sin_t[:, :, None]
    turned_real = section_real * cos_t + section_imag * sin_t
    turned_imag = section_imag * cos_t - section_real * sin_t
    cos_b, sin_b = angle_tables(inner_len, start, count, inner_len)
    out_real = exact_einsum("qb,fkbm->fqkm", cos_b, turned_real) + exact_einsum(
        "qb,fkbm->fqkm", sin_b, turned_imag
    )
    out_imag = exact_einsum("qb,fkbm->fqkm", cos_b, turned_imag) - exact_einsum(
        "qb,fkbm->fqkm", sin_b, turned_real
    )
    return (out_real.reshape(fields, length, slots), out_imag.reshape(fields, length, slots))


def accumulate(spectrum_block, table_block, spin_block, length, ell_index):
    count = table_block.shape[0]
    positions = jnp.arange(count, dtype=jnp.int32)
    freq = jnp.where(positions < length // 2, positions, positions - length)
    terms = []
    for degree in range(table_block.shape[1]):
        keep_rows = (jnp.abs(freq) <= ell_index[degree]).astype(jnp.float32)
        row_weights = spin_block[:, :, degree].astype(jnp.float32).T * keep_rows[None, :]
        table = table_block[:, degree, :].astype(jnp.float32)
        terms.append(
            jnp.einsum(
                "fk,ks,xfks->fxs",
                row_weights,
                table,
                spectrum_block,
                precision=lax.Precision.HIGHEST,
            )
        )
    return jnp.stack(terms)


def on_device(maps, deltas, spin_rows, ell_index, owner_map, prior):
    theta_count = lax.axis_size("theta")
    phi_count = lax.axis_size("phi")
    length = maps.shape[2] * phi_count
    values = maps.astype(jnp.float32)
    planes = jnp.stack([values[0], values[1] * values[2], values[1] * values[3]])
    row_planes = lax.all_to_all(planes, "phi", split_axis=1, concat_axis=2, tiled=True)
    inner_len = length // theta_count
    spectra = [
        row_transform(row_planes[0], None, theta_count, inner_len),
        row_transform(row_planes[1], row_planes[2], theta_count, inner_len),
    ]
    stacked = jnp.stack(
        [
            jnp.stack([spectrum[0] for spectrum in spectra]),
            jnp.stack([spectrum[1] for spectrum in spectra]),
        ]
    )
    permuted = jnp.take(stacked, owner_map, axis=3)
    columns = lax.all_to_all(permuted, "theta", split_axis=3, concat_axis=2, tiled=True)
    fields = columns.shape[1]
    slots = columns.shape[3]
    sub_rows = columns.shape[2] // theta_count
    blocks = columns.reshape(2, fields, theta_count, sub_rows, slots)
    row_start = lax.axis_index("phi") * sub_rows
    spec_real, spec_imag = column_transform(blocks[0], blocks[1], theta_count, inner_len, row_start)
    combined = jnp.stack([spec_real, spec_imag])
    totals = accumulate(
        combined,
        lax.all_gather(deltas, "phi", axis=0, tiled=True),
        lax.all_gather(spin_rows, "phi", axis=0, tiled=True),
        length,
        ell_index,
    )
    shares = lax.psum_scatter(totals, "phi", scatter_dimension=3, tiled=True)
    share_count = shares.shape[3]
    slot_start = lax.axis_index("theta") * slots + lax.axis_index("phi") * share_count
    share_ids = lax.dynamic_slice_in_dim(owner_map, slot_start, share_count)
    slot_freq = jnp.where(share_ids < length // 2, share_ids, share_ids - length)
    ell_float = ell_index.astype(jnp.float32)
    weight = 2.0 * math.pi / length * jnp.sqrt((2.0 * ell_float + 1.0) / (4.0 * math.pi)) / length
    keep_slots = (jnp.abs(slot_freq)[None, :] <= ell_index[:, None]).astype(jnp.float32) * weight[
        :, None
    ]
    scalar_real = shares[:, 0, 0] * keep_slots
    scalar_imag = shares[:, 0, 1] * keep_slots
    spin_real = shares[:, 1, 0] * keep_slots
    spin_imag = shares[:, 1, 1] * keep_slots
    coupling = (prior * jnp.sqrt(ell_float * (ell_float + 1.0)) / (length // 2))[:, None]
    inner_real = -spin_imag - coupling * scalar_real
    inner_imag = spin_real - coupling * scalar_imag
    turns = jnp.mod(-slot_freq, 4)
    phase_real = jnp.where(turns == 0, 1.0, jnp.where(turns == 2, -1.0, 0.0)).astype(jnp.float32)[
        None, :
    ]
    phase_imag = jnp.where(turns == 1, 1.0, jnp.where(turns == 3, -1.0, 0.0)).astype(jnp.float32)[
        None, :
    ]
    out_real = phase_real * inner_real - phase_imag * inner_imag
    out_imag = phase_real * inner_imag + phase_imag * inner_real
    return jnp.stack([out_real, out_imag], axis=1)


def solution(mesh):
    placed = (
        P("grp", "theta", "phi"),
        P("phi", None, "theta"),
        P("phi", None, None),
        P(),
        P(),
        P(),
    )
    return jax.shard_map(
        on_device,
        mesh=mesh,
        in_specs=placed,
        out_specs=P("grp", None, ("theta", "phi")),
        check_vma=False,
    )
```

profile of v0, /device:TPU:0, one launch (start us, length us, event | category | flops | bytes accessed | tf_op | source)
XLA Modules:
  0.0 1105.6 jit_solution(13020259938788177995)
XLA Ops:
  6.5 11.3 %convert_element_type.145 = f32[4,512,2048]{2,1,0:T(8,128)} convert(bf16[4,512,2048]{2,1,0:T(8,128)(2,1)} %param.6) | non-fusion elementwise | flops 4194304 | bytes 25165824 | tf_op jit(solution)/shard_map/convert_element_type | solution.py:100
  22.0 8.4 slice_multiply_fusion.1
  30.3 9.8 pad_maximum_fusion.1
  40.1 16.7 %copy.115 = f32[3,512,2048]{2,0,1:T(4,128)S(1)} copy(f32[3,512,2048]{2,1,0:T(8,128)} %pad_maximum_fusion.1) | data formatting | bytes 25165824 | tf_op jit(solution)/shard_map/stack | solution.py:101
  56.8 17.4 %all_to_all.30 = f32[3,512,2048]{2,0,1:T(4,128)S(1)} all-to-all(f32[3,512,2048]{2,0,1:T(4,128)S(1)} %copy.115), channel_id=1, replica_groups=mesh['grp'=2,'theta'=8,'phi'=2] {'phi'}, dimensions={1} | all-to-all | bytes 25165824 | tf_op jit(solution)/shard_map/all_to_all | solution.py:102
  74.2 14.4 %copy.241 = f32[3,2,256,2048]{3,1,2,0:T(2,128)} copy(f32[3,2,256,2048]{3,0,2,1:T(4,128)S(1)} %bitcast.262) | data formatting | bytes 25165824 | tf_op jit(solution)/shard_map/all_to_all | solution.py:102
  88.6 8.9 fusion.248
  104.0 8.7 fusion.126
  124.7 10.2 negate_add_fusion
  146.8 8.6 fusion.129
  155.5 10.5 fusion.24
  166.0 13.1 %fusion.36 = f32[256,8,512]{2,0,1:T(8,128)S(1)} fusion(f32[256,8,512]{2,1,0:T(8,128)S(1)} %get-tuple-element.26), kind=kOutput, calls=%fused_computation.77 | convolution fusion | flops 6446120960 | bytes 8388608 | tf_op jit(solution)/shard_map/qb,rkb->rqk/dot_general | solution.py:9
  179.0 15.6 %fusion.34 = f32[256,8,512]{2,0,1:T(8,128)} fusion(f32[256,8,512]{2,1,0:T(8,128)S(1)} %get-tuple-element.26), kind=kOutput, calls=%fused_computation.75 | convolution fusion | flops 6446120960 | bytes 8388608 | tf_op jit(solution)/shard_map/qb,rkb->rqk/dot_general | solution.py:9
  194.6 15.8 %fusion.28 = f32[256,8,512]{2,0,1:T(8,128)} fusion(f32[256,8,512]{2,1,0:T(8,128)S(1)} %get-tuple-element.37), kind=kOutput, calls=%fused_computation.69 | convolution fusion | flops 6446120960 | bytes 8388608 | tf_op jit(solution)/shard_map/qb,rkb->rqk/dot_general | solution.py:9
  210.4 16.0 %fusion.26 = f32[256,8,512]{2,0,1:T(8,128)} fusion(f32[256,8,512]{2,1,0:T(8,128)S(1)} %get-tuple-element.37), kind=kOutput, calls=%fused_computation.67 | convolution fusion | flops 6446120960 | bytes 8388608 | tf_op jit(solution)/shard_map/qb,rkb->rqk/dot_general | solution.py:9
  226.5 15.9 %add_bitcast_fusion.2 = f32[256,512,8]{1,0,2:T(8,128)} fusion(f32[256,8,512]{2,0,1:T(8,128)S(1)} %fusion.36, f32[256,8,512]{2,1,0:T(8,128)S(1)} %get-tuple-element.25), kind=kOutput, calls=%fused_computation.66 | convolution fusion | flops 6447169536 | bytes 12582912 | tf_op jit(solution)/shard_map/qb,rkb->rqk/dot_general | solution.py:9
  247.8 9.5 copy.123
  257.3 15.8 %add_bitcast_fusion.1 = f32[256,512,8]{1,0,2:T(8,128)} fusion(f32[256,8,512]{2,0,1:T(8,128)S(1)} %copy-done.13, f32[256,8,512]{2,1,0:T(8,128)S(1)} %copy-done.4), kind=kOutput, calls=%fused_computation.64 | convolution fusion | flops 6447169536 | bytes 12582912 | tf_op jit(solution)/shard_map/qb,rkb->rqk/dot_general | solution.py:9
  278.6 9.5 copy.124
  288.1 16.1 %subtract_bitcast_fusion.2 = f32[256,512,8]{1,0,2:T(8,128)} fusion(f32[256,8,512]{2,0,1:T(8,128)S(1)} %copy-done.12, f32[256,8,512]{2,1,0:T(8,128)S(1)} %copy-done.7), kind=kOutput, calls=%fused_computation.63 | convolution fusion | flops 6447169536 | bytes 12582912 | tf_op jit(solution)/shard_map/qb,rkb->rqk/dot_general | solution.py:9
  309.7 9.5 copy.131
  319.1 15.8 %subtract_bitcast_fusion.1 = f32[256,512,8]{1,0,2:T(8,128)} fusion(f32[256,8,512]{2,0,1:T(8,128)S(1)} %copy-done.11, f32[256,8,512]{2,1,0:T(8,128)S(1)} %copy-done.5), kind=kOutput, calls=%fused_computation.62 | convolution fusion | flops 6447169536 | bytes 12582912 | tf_op jit(solution)/shard_map/qb,rkb->rqk/dot_general | solution.py:9
  340.4 7.9 copy.132
  363.8 8.6 pad_maximum_fusion
  372.4 52.5 %gather_fusion = f32[4096,2,2,256]{3,2,1,0:T(2,128)} fusion(f32[2,2,256,4096]{2,1,3,0:T(2,128)} %pad_maximum_fusion, s32[4096]{0:T(1024)S(1)} %fusion.105), kind=kCustom, calls=%fused_computation | custom fusion | bytes 33570816 | tf_op jit(solution)/shard_map/jit(_take)/gather | solution.py:114
  424.9 17.6 %select_bitcast_fusion = f32[2,2,256,4096]{2,1,0,3:T(2,128)} fusion(f32[4096,2,2,256]{3,2,1,0:T(2,128)} %gather_fusion, pred[4096]{0:T(1024)(128)(4,1)S(1)} %compare_and_fusion), kind=kLoop, calls=%fused_computation.9 | loop fusion | flops 4194304 | bytes 33558528 | tf_op jit(solution)/shard_map/jit(_take)/select_n | solution.py:114
  449.8 8.4 copy.114
  472.9 17.0 %all-gather.2.cloned.1.call-done = bf16[4096,4,512]{2,0,1:T(8,128)(2,1)} async-done(((bf16[2048,4,512]{2,0,1:T(8,128)(2,1)}), bf16[4096,4,512]{2,0,1:T(8,128)(2,1)}) %all-gather.2.cloned.1.call-update) | async-done | bytes 16777232 | tf_op jit(solution)/shard_map/all_gather | solution.py:125
  489.9 15.4 %fusion.18 = (f32[4096,512]{1,0:T(8,128)}, f32[4096,512]{1,0:T(8,128)}, f32[4096,512]{1,0:T(8,128)}, f32[4096,512]{1,0:T(8,128)}) fusion(bf16[4096,4,512]{2,0,1:T(8,128)(2,1)} %all-gather.2.cloned.1.call-done), kind=kLoop, calls=%fused_computation.41 | loop fusion | flops 8388608 | bytes 50331648 | tf_op jit(solution)/shard_map/convert.15
  505.3 20.2 %multiply_bitcast_fusion = (f32[2,512,4096]{1,0,2:T(2,128)}, f32[2,512,4096]{1,0,2:T(2,128)}) fusion(f32[4096,512]{1,0:T(8,128)} %get-tuple-element.16, f32[4096,2]{1,0:T(8,128)} %copy.144, f32[4096,512]{1,0:T(8,128)} %get-tuple-element.17, f32[4096,2]{1,0:T(8,128)S(1)} %copy.143), kind=kLoop, calls=%fused_computation.10 | loop fusion | flops 8388608 | bytes 50397184
  525.4 15.2 %copy.190 = f32[2,512,4096]{1,2,0:T(8,128)} copy(f32[2,512,4096]{1,0,2:T(2,128)} %get-tuple-element.48) | data formatting | bytes 33554432
  541.9 8.9 copy.191
  550.8 20.1 %multiply_bitcast_fusion.2 = (f32[2,512,4096]{1,0,2:T(2,128)}, f32[2,512,4096]{1,0,2:T(2,128)}) fusion(f32[4096,512]{1,0:T(8,128)} %get-tuple-element.18, f32[4096,2]{1,0:T(8,128)} %copy.142, f32[4096,512]{1,0:T(8,128)} %get-tuple-element.19, f32[4096,2]{1,0:T(8,128)S(1)} %copy-done.18), kind=kLoop, calls=%fused_computation.12 | loop fusion | flops 8388608 | bytes 50397184
  571.0 15.2 %copy.188 = f32[2,512,4096]{1,2,0:T(8,128)} copy(f32[2,512,4096]{1,0,2:T(2,128)} %get-tuple-element.50) | data formatting | bytes 33554432
  587.4 8.8 copy.189
  596.3 216.9 %all-to-all-done.1 = f32[2,2,256,4096]{2,1,0,3:T(2,128)} async-done(((f32[2,2,256,4096]{2,1,0,3:T(2,128)}), f32[2,2,256,4096]{2,1,0,3:T(2,128)}, u32[]{:S(2)}, u32[]{:S(2)}) %all-to-all-start.1) | async-done | bytes 16777248 | tf_op jit(solution)/shard_map/all_to_all | solution.py:115
  813.2 19.4 %copy.177 = f32[2,2,256,8,512]{4,3,2,1,0:T(8,128)} copy(f32[2,2,256,8,512]{2,1,0,4,3:T(2,128)} %bitcast.33) | data formatting | bytes 33554432 | tf_op jit(solution)/shard_map/all_to_all | solution.py:115
  832.6 11.8 %fusion.2 = f32[2,256,512,8]{2,3,1,0:T(8,128)} fusion(f32[2,2,8,256,512]{4,2,3,1,0:T(8,128)} %bitcast.258), kind=kOutput, calls=%fused_computation.28 | convolution fusion | flops 201327488 | bytes 16777216 | tf_op jit(solution)/shard_map/ka,fabm->fkbm/dot_general | solution.py:9
  844.4 9.4 fusion.3
  853.8 9.4 fusion.5
  863.2 21.9 %fusion = (f32[2,8,256,512]{3,1,2,0:T(8,128)}, f32[2,8,256,512]{3,1,2,0:T(8,128)}) fusion(f32[8,256]{0,1:T(8,128)S(1)} %copy.135, f32[8,256]{0,1:T(8,128)S(1)} %copy.134, f32[2,256,512,8]{2,3,1,0:T(8,128)} %fusion.2, f32[2,256,512,8]{2,3,1,0:T(8,128)} %fusion.3, f32[2,256,512,8]{2,3,1,0:T(8,128)} %fusion.5, f32[2,2,8,256,512]{4,2,3,1,0:T(8,128)} %bitcast.259), kind=kOutput, calls=%fused_computation.24 | convolution fusion | flops 218104704 | bytes 50348032 | tf_op jit(solution)/shard_map/ka,fabm->fkbm/dot_general | solution.py:9
  885.1 26.0 %fusion.8 = f32[2,8,512,512]{2,3,1,0:T(8,128)} fusion(f32[2,8,256,512]{3,1,2,0:T(8,128)} %get-tuple-element.15, s32[256]{0:T(256)S(1)} %iota_add_fusion), kind=kOutput, calls=%fused_computation.34 | convolution fusion | flops 12886736896 | bytes 25166848 | tf_op jit(solution)/shard_map/qb,fkbm->fqkm/dot_general | solution.py:9
  911.1 25.8 %fusion.6 = f32[2,8,512,512]{2,3,1,0:T(8,128)S(1)} fusion(f32[2,8,256,512]{3,1,2,0:T(8,128)} %get-tuple-element.15, s32[256]{0:T(256)S(1)} %iota_add_fusion), kind=kOutput, calls=%fused_computation.32 | convolution fusion | flops 12886736896 | bytes 25166848 | tf_op jit(solution)/shard_map/qb,fkbm->fqkm/dot_general | solution.py:9
  936.9 49.7 %add_bitcast_fusion = f32[2,512,8,512]{3,1,2,0:T(8,128)} fusion(f32[2,8,512,512]{2,3,1,0:T(8,128)} %fusion.8, f32[2,8,256,512]{3,1,2,0:T(8,128)} %get-tuple-element.14, s32[256]{0:T(256)S(1)} %iota_add_fusion), kind=kOutput, calls=%fused_computation.14 | convolution fusion | flops 12890931200 | bytes 41944064 | tf_op jit(solution)/shard_map/qb,fkbm->fqkm/dot_general | solution.py:9
  986.6 17.7 %copy.240 = f32[2,512,8,512]{3,2,1,0:T(8,128)} copy(f32[2,512,8,512]{3,1,2,0:T(8,128)} %add_bitcast_fusion) | data formatting | bytes 33554432 | tf_op jit(solution)/shard_map/add | solution.py:66
  1004.4 27.7 %subtract_bitcast_fusion = f32[2,512,8,512]{3,1,2,0:T(8,128)} fusion(f32[2,8,512,512]{2,3,1,0:T(8,128)S(1)} %fusion.6, f32[2,8,256,512]{3,1,2,0:T(8,128)} %get-tuple-element.14, s32[256]{0:T(256)S(1)} %iota_add_fusion), kind=kOutput, calls=%fused_computation.13 | convolution fusion | flops 12890931200 | bytes 41944064 | tf_op jit(solution)/shard_map/qb,fkbm->fqkm/dot_general | solution.py:9
  1032.1 19.3 %copy.239 = f32[2,512,8,512]{3,2,1,0:T(8,128)} copy(f32[2,512,8,512]{3,1,2,0:T(8,128)} %subtract_bitcast_fusion) | data formatting | bytes 33554432 | tf_op jit(solution)/shard_map/sub | solution.py:69
  1051.5 27.6 %multiply_reduce_fusion.3 = (f32[2,512,2]{1,0,2:T(2,128)S(1)}, f32[2,512,2]{1,0,2:T(2,128)S(1)}, f32[2,512,2]{1,0,2:T(2,128)S(1)}, f32[2,512,2]{1,0,2:T(2,128)S(1)}) fusion(f32[2,512,4096]{1,2,0:T(8,128)} %copy.188, f32[1,2,4096,512]{3,2,1,0:T(8,128)} %bitcast.264, f32[1,2,4096,512]{3,2,1,0:T(8,128)S(1)} %bitcast.263, f32[2,512,4096]{1,2,0:T(8,128)} %copy.189, ...), kind=kLoop, calls=%fused_computation.5 | loop fusion | flops 75489280 | bytes 100696064 | tf_op jit(solution)/shard_map/fk,ks,xfks->fxs/dot_general | solution.py:85
  (112 shorter events, 115.7 us)
Async XLA Ops:
  104.0 8.7 copy-start.10
  124.7 10.2 copy-start.8
  124.7 10.2 copy-start.14
  146.8 8.6 copy-start.9
  165.9 60.5 %copy-start.6 = (f32[256,8,512]{2,1,0:T(8,128)}, f32[256,8,512]{2,1,0:T(8,128)S(1)}, u32[]{:S(2)}) copy-start(f32[256,8,512]{2,1,0:T(8,128)S(1)} %get-tuple-element.25) | copy-start | bytes 12582916
  194.6 31.8 %copy-start.19 = (s32[4096]{0:T(1024)S(1)}, s32[4096]{0:T(1024)}, u32[]{:S(2)}) copy-start(s32[4096]{0:T(1024)} %param.10) | copy-start | bytes 49156
  247.8 9.5 copy-start.4
  247.8 9.5 copy-start.13
  278.6 9.5 copy-start.7
  278.6 9.5 copy-start.12
  309.6 9.5 copy-start.5
  309.6 9.5 copy-start.11
  340.4 7.9 copy-start.15
  340.4 7.9 copy-start.16
  348.3 7.7 copy-start.17
  442.5 370.7 %all-to-all-start.1 = ((f32[2,2,256,4096]{2,1,0,3:T(2,128)}), f32[2,2,256,4096]{2,1,0,3:T(2,128)}, u32[]{:S(2)}, u32[]{:S(2)}) async-start(f32[2,2,256,4096]{2,1,0,3:T(2,128)} %select_bitcast_fusion), calls=%async_computation.1 | async-start | bytes 33554432 | tf_op jit(solution)/shard_map/all_to_all | solution.py:115
  449.8 40.1 %all-gather.2.cloned.1.call-start = ((), (), s32[]{:S(2)}) async-start(), calls=%async_computation.3 | async-start | bytes 25165824 | tf_op jit(solution)/shard_map/all_gather | solution.py:125
  458.2 0.8 copy-start.20
  458.2 2.6 copy-start.21
  458.2 14.1 %copy-start.27 = (f32[4]{0:T(128)S(1)}, f32[4]{0:T(128)}, u32[]{:S(2)}) copy-start(f32[4]{0:T(128)} %param.11) | copy-start | bytes 52
  458.3 632.6 %reduce-scatter.4.cloned.1.call-start = ((), (), s32[]{:S(2)}) async-start(), calls=%async_computation.4 | async-start | bytes 393216
  525.4 16.5 %copy-start.1 = (f32[2,512,4096]{1,0,2:T(2,128)S(1)}, f32[2,512,4096]{1,0,2:T(2,128)}, u32[]{:S(2)}) copy-start(f32[2,512,4096]{1,0,2:T(2,128)} %get-tuple-element.47) | copy-start | bytes 50331652
  541.9 8.9 copy-start.18
  570.9 16.5 %copy-start.2 = (f32[2,512,4096]{1,0,2:T(2,128)S(1)}, f32[2,512,4096]{1,0,2:T(2,128)}, u32[]{:S(2)}) copy-start(f32[2,512,4096]{1,0,2:T(2,128)} %get-tuple-element.49) | copy-start | bytes 50331652
  832.6 11.8 %copy-start = (f32[2,2,256,8,512]{4,3,2,1,0:T(8,128)S(1)}, f32[2,2,256,8,512]{4,3,2,1,0:T(8,128)}, u32[]{:S(2)}) copy-start(f32[2,2,256,8,512]{4,3,2,1,0:T(8,128)} %copy.177) | copy-start | bytes 50331652
  1032.1 19.4 %copy-start.3 = (f32[2,512,8,512]{3,2,1,0:T(8,128)S(1)}, f32[2,512,8,512]{3,2,1,0:T(8,128)}, u32[]{:S(2)}) copy-start(f32[2,512,8,512]{3,2,1,0:T(8,128)} %copy.240) | copy-start | bytes 50331652
  1079.1 18.7 %copy-start.22 = (s32[4]{0:T(128)S(1)}, s32[4]{0:T(128)}, u32[]{:S(2)}) copy-start(s32[4]{0:T(128)} %param.9) | copy-start | bytes 52
  1079.1 18.7 %copy-start.23 = (f32[256]{0:T(256)S(1)}, f32[256]{0:T(256)}, u32[]{:S(2)}) copy-start(f32[256]{0:T(256)} %get-tuple-element.12) | copy-start | bytes 3076
  1079.1 18.7 %copy-start.24 = (f32[256]{0:T(256)S(1)}, f32[256]{0:T(256)}, u32[]{:S(2)}) copy-start(f32[256]{0:T(256)} %compare_select_fusion.7) | copy-start | bytes 3076
  1079.1 18.7 %copy-start.25 = (f32[4]{0:T(128)S(1)}, f32[4]{0:T(128)}, u32[]{:S(2)}) copy-start(f32[4]{0:T(128)} %get-tuple-element.41) | copy-start | bytes 52
  1079.1 18.7 %copy-start.26 = (f32[4]{0:T(128)S(1)}, f32[4]{0:T(128)}, u32[]{:S(2)}) copy-start(f32[4]{0:T(128)} %get-tuple-element.42) | copy-start | bytes 52
Sparse Core Ops, SparseCore 0:
  458.4 31.4 all-gather.1
  1084.0 6.7 reduce-scatter.3
where the time goes:
time: 1110 us
  matrix products  354 us (32%)
  local copies, waits for them, and re-layouts  310 us (28%)
  waiting for transfers between devices  240 us (22%)
  other arithmetic  161 us (15%)
  blocking collectives  19.2 us (2%)
  between operations  14.1 us (1%)
    dot_general x22, matrix products, exact_einsum(): return jnp.einsum(form, table, operand, precision=lax.Precision.HIGHEST)  354 us
    all_to_all x1, waiting for transfers between devices, on_device(): lax.all_to_all(permuted, 'theta', split_axis=3, concat_axis=2, tiled=True)  217 us
    unnamed x68, local copies, waits for them, and re-layouts  68.2 us
    gather x1, local copies, waits for them, and re-layouts, on_device(): permuted = jnp.take(stacked, owner_map, axis=3)  52.5 us
    unnamed x2, other arithmetic  40.3 us
    dot_general x1, other arithmetic, accumulate(): jnp.einsum('fk,ks,xfks->fxs', row_weights, table, spectrum_block, precisi...  27.6 us
    another operation x3, other arithmetic, on_device(): jnp.stack([jnp.stack([spectrum[0] for spectrum in spectra]), jnp.stack([s...  24 us
  transfers between devices with their start and end apart: 3, of which 3 were waited for; matrix products, arithmetic and copies ran while one was open for 11% of the time, Pallas kernels for 0%

commit v1 on v0

--- a/solution.py
+++ b/solution.py
@@ -3,6 +3,7 @@
 import jax.numpy as jnp
 from jax import lax
 from jax.sharding import PartitionSpec as P
+from jax.lax import all_to_all, axis_size
 
 
 def exact_einsum(form, table, operand):
@@ -112,7 +113,16 @@
         ]
     )
     permuted = jnp.take(stacked, owner_map, axis=3)
-    columns = lax.all_to_all(permuted, "theta", split_axis=3, concat_axis=2, tiled=True)
+    _post_plane = lambda q_in: jnp.concatenate(
+        all_to_all(
+            jnp.stack(jnp.split(q_in, axis_size("theta"), 3)),
+            axis_name="theta",
+            split_axis=0,
+            concat_axis=0,
+        ),
+        axis=2,
+    )
+    columns = _post_plane(permuted)
     fields = columns.shape[1]
     slots = columns.shape[3]
     sub_rows = columns.shape[2] // theta_count

time: 1110 us -> 1150 us (1.036)
  local copies, waits for them, and re-layouts: 310 us -> 347 us
    another operation x0 -> x2, local copies, waits for them, and re-layouts: none -> 27.1 us  [on_device(): jnp.stack(jnp.split(q_in, axis_size('theta'), 3))]
    unnamed x68 -> x75, local copies, waits for them, and re-layouts: 68.2 us -> 82.8 us
where the time goes in v1:
time: 1150 us; the launch traced here: 1140 us
  matrix products  352 us (31%)
  local copies, waits for them, and re-layouts  347 us (30%)
  waiting for transfers between devices  240 us (21%)
  other arithmetic  160 us (14%)
  blocking collectives  19.2 us (2%)
  between operations  14.1 us (1%)
    dot_general x22, matrix products, exact_einsum(): return jnp.einsum(form, table, operand, precision=lax.Precision.HIGHEST)  352 us
    all_to_all x1, waiting for transfers between devices, on_device(): all_to_all(jnp.stack(jnp.split(q_in, axis_size('theta'), 3)), axis_name='...  217 us
    unnamed x75, local copies, waits for them, and re-layouts  82.8 us
    gather x1, local copies, waits for them, and re-layouts, on_device(): permuted = jnp.take(stacked, owner_map, axis=3)  52.4 us
    unnamed x2, other arithmetic  40.3 us
    dot_general x1, other arithmetic, accumulate(): jnp.einsum('fk,ks,xfks->fxs', row_weights, table, spectrum_block, precisi...  27.6 us
    another operation x2, local copies, waits for them, and re-layouts, on_device(): jnp.stack(jnp.split(q_in, axis_size('theta'), 3))  27.1 us
    another operation x3, other arithmetic, on_device(): jnp.stack([jnp.stack([spectrum[0] for spectrum in spectra]), jnp.stack([s...  24.1 us
  transfers between devices with their start and end apart: 3, of which 3 were waited for; matrix products, arithmetic and copies ran while one was open for 11% of the time, Pallas kernels for 0%

profile of v1, /device:TPU:0, one launch (start us, length us, event | category | flops | bytes accessed | tf_op | source)
XLA Modules:
  0.0 1139.7 jit_solution(17851256556611671881)
XLA Ops:
  6.5 11.3 convert_element_type.145
  22.0 8.4 slice_multiply_fusion.1
  30.3 9.8 pad_maximum_fusion.1
  40.1 16.7 %copy.131 = f32[3,512,2048]{2,0,1:T(4,128)S(1)} copy(f32[3,512,2048]{2,1,0:T(8,128)} %pad_maximum_fusion.1) | data formatting | bytes 25165824 | tf_op jit(solution)/shard_map/stack | solution.py:102
  56.8 17.4 %all_to_all.20 = f32[3,512,2048]{2,0,1:T(4,128)S(1)} all-to-all(f32[3,512,2048]{2,0,1:T(4,128)S(1)} %copy.131), channel_id=1, replica_groups=mesh['grp'=2,'theta'=8,'phi'=2] {'phi'}, dimensions={1} | all-to-all | bytes 25165824 | tf_op jit(solution)/shard_map/all_to_all | solution.py:103
  74.2 14.4 %copy.259 = f32[3,2,256,2048]{3,1,2,0:T(2,128)} copy(f32[3,2,256,2048]{3,0,2,1:T(4,128)S(1)} %bitcast.295) | data formatting | bytes 25165824 | tf_op jit(solution)/shard_map/all_to_all | solution.py:103
  88.6 8.9 fusion.256
  104.0 8.7 fusion.134
  124.7 10.2 negate_add_fusion
  146.8 8.6 fusion.137
  155.5 10.5 fusion.24
  166.0 13.1 %fusion.36 = f32[256,8,512]{2,0,1:T(8,128)S(1)} fusion(f32[256,8,512]{2,1,0:T(8,128)S(1)} %get-tuple-element.26), kind=kOutput, calls=%fused_computation.78 | convolution fusion | flops 6446120960 | bytes 8388608 | tf_op jit(solution)/shard_map/qb,rkb->rqk/dot_general | solution.py:10
  179.0 15.6 %fusion.34 = f32[256,8,512]{2,0,1:T(8,128)} fusion(f32[256,8,512]{2,1,0:T(8,128)S(1)} %get-tuple-element.26), kind=kOutput, calls=%fused_computation.76 | convolution fusion | flops 6446120960 | bytes 8388608 | tf_op jit(solution)/shard_map/qb,rkb->rqk/dot_general | solution.py:10
  194.6 15.8 %fusion.28 = f32[256,8,512]{2,0,1:T(8,128)} fusion(f32[256,8,512]{2,1,0:T(8,128)S(1)} %get-tuple-element.37), kind=kOutput, calls=%fused_computation.70 | convolution fusion | flops 6446120960 | bytes 8388608 | tf_op jit(solution)/shard_map/qb,rkb->rqk/dot_general | solution.py:10
  210.4 16.0 %fusion.26 = f32[256,8,512]{2,0,1:T(8,128)} fusion(f32[256,8,512]{2,1,0:T(8,128)S(1)} %get-tuple-element.37), kind=kOutput, calls=%fused_computation.68 | convolution fusion | flops 6446120960 | bytes 8388608 | tf_op jit(solution)/shard_map/qb,rkb->rqk/dot_general | solution.py:10
  226.5 15.9 %add_bitcast_fusion.2 = f32[256,512,8]{1,0,2:T(8,128)} fusion(f32[256,8,512]{2,0,1:T(8,128)S(1)} %fusion.36, f32[256,8,512]{2,1,0:T(8,128)S(1)} %get-tuple-element.25), kind=kOutput, calls=%fused_computation.67 | convolution fusion | flops 6447169536 | bytes 12582912 | tf_op jit(solution)/shard_map/qb,rkb->rqk/dot_general | solution.py:10
  247.8 9.5 copy.139
  257.3 15.8 %add_bitcast_fusion.1 = f32[256,512,8]{1,0,2:T(8,128)} fusion(f32[256,8,512]{2,0,1:T(8,128)S(1)} %copy-done.13, f32[256,8,512]{2,1,0:T(8,128)S(1)} %copy-done.4), kind=kOutput, calls=%fused_computation.65 | convolution fusion | flops 6447169536 | bytes 12582912 | tf_op jit(solution)/shard_map/qb,rkb->rqk/dot_general | solution.py:10
  278.6 9.5 copy.140
  288.1 16.1 %subtract_bitcast_fusion.2 = f32[256,512,8]{1,0,2:T(8,128)} fusion(f32[256,8,512]{2,0,1:T(8,128)S(1)} %copy-done.12, f32[256,8,512]{2,1,0:T(8,128)S(1)} %copy-done.7), kind=kOutput, calls=%fused_computation.64 | convolution fusion | flops 6447169536 | bytes 12582912 | tf_op jit(solution)/shard_map/qb,rkb->rqk/dot_general | solution.py:10
  309.7 9.5 copy.147
  319.1 15.8 %subtract_bitcast_fusion.1 = f32[256,512,8]{1,0,2:T(8,128)} fusion(f32[256,8,512]{2,0,1:T(8,128)S(1)} %copy-done.11, f32[256,8,512]{2,1,0:T(8,128)S(1)} %copy-done.5), kind=kOutput, calls=%fused_computation.63 | convolution fusion | flops 6447169536 | bytes 12582912 | tf_op jit(solution)/shard_map/qb,rkb->rqk/dot_general | solution.py:10
  363.8 8.6 pad_maximum_fusion
  372.4 52.4 %gather_fusion = f32[4096,2,2,256]{3,2,1,0:T(2,128)} fusion(f32[2,2,256,4096]{2,1,3,0:T(2,128)} %pad_maximum_fusion, s32[4096]{0:T(1024)S(1)} %fusion.113), kind=kCustom, calls=%fused_computation | custom fusion | bytes 33570816 | tf_op jit(solution)/shard_map/jit(_take)/gather | solution.py:115
  424.8 16.4 %select_bitcast_fusion = f32[2,2,256,4096]{2,1,0,3:T(2,128)S(1)} fusion(f32[4096,2,2,256]{3,2,1,0:T(2,128)} %gather_fusion, pred[4096]{0:T(1024)(128)(4,1)S(1)} %compare_and_fusion), kind=kLoop, calls=%fused_computation.10 | loop fusion | flops 4194304 | bytes 33558528 | tf_op jit(solution)/shard_map/jit(_take)/select_n | solution.py:115
  457.9 25.0 %copy.149 = f32[8,2,2,256,512]{4,3,2,1,0:T(8,128)} copy(f32[8,2,2,256,512]{3,2,1,4,0:T(2,128)} %fusion.50) | data formatting | bytes 33554432 | tf_op jit(solution)/shard_map/stack | solution.py:118
  490.2 8.4 copy.130
  513.3 17.0 %all-gather.2.cloned.1.call-done = bf16[4096,4,512]{2,0,1:T(8,128)(2,1)} async-done(((bf16[2048,4,512]{2,0,1:T(8,128)(2,1)}), bf16[4096,4,512]{2,0,1:T(8,128)(2,1)}) %all-gather.2.cloned.1.call-update) | async-done | bytes 16777232 | tf_op jit(solution)/shard_map/all_gather | solution.py:135
  530.3 15.8 %fusion.18 = (f32[4096,512]{1,0:T(8,128)}, f32[4096,512]{1,0:T(8,128)}, f32[4096,512]{1,0:T(8,128)}, f32[4096,512]{1,0:T(8,128)}) fusion(bf16[4096,4,512]{2,0,1:T(8,128)(2,1)} %all-gather.2.cloned.1.call-done), kind=kLoop, calls=%fused_computation.42 | loop fusion | flops 8388608 | bytes 50331648 | tf_op jit(solution)/shard_map/convert.15
  546.0 20.2 %multiply_bitcast_fusion = (f32[2,512,4096]{1,0,2:T(2,128)}, f32[2,512,4096]{1,0,2:T(2,128)}) fusion(f32[4096,512]{1,0:T(8,128)} %get-tuple-element.16, f32[4096,2]{1,0:T(8,128)} %copy.161, f32[4096,512]{1,0:T(8,128)} %get-tuple-element.17, f32[4096,2]{1,0:T(8,128)S(1)} %copy.160), kind=kLoop, calls=%fused_computation.11 | loop fusion | flops 8388608 | bytes 50397184
  566.2 15.2 %copy.206 = f32[2,512,4096]{1,2,0:T(8,128)} copy(f32[2,512,4096]{1,0,2:T(2,128)} %get-tuple-element.48) | data formatting | bytes 33554432
  582.7 8.9 copy.207
  591.6 20.1 %multiply_bitcast_fusion.2 = (f32[2,512,4096]{1,0,2:T(2,128)}, f32[2,512,4096]{1,0,2:T(2,128)}) fusion(f32[4096,512]{1,0:T(8,128)} %get-tuple-element.18, f32[4096,2]{1,0:T(8,128)} %copy.159, f32[4096,512]{1,0:T(8,128)} %get-tuple-element.19, f32[4096,2]{1,0:T(8,128)S(1)} %copy-done.18), kind=kLoop, calls=%fused_computation.13 | loop fusion | flops 8388608 | bytes 50397184
  611.7 15.2 %copy.204 = f32[2,512,4096]{1,2,0:T(8,128)} copy(f32[2,512,4096]{1,0,2:T(2,128)} %get-tuple-element.50) | data formatting | bytes 33554432
  628.2 8.8 copy.205
  637.1 216.5 %all-to-all-done.1 = f32[8,2,2,256,512]{4,3,2,1,0:T(8,128)} async-done(((f32[8,2,2,256,512]{4,3,2,1,0:T(8,128)}), f32[8,2,2,256,512]{4,3,2,1,0:T(8,128)}, u32[]{:S(2)}, u32[]{:S(2)}) %all-to-all-start.1) | async-done | bytes 16777248 | tf_op jit(solution)/shard_map/all_to_all | solution.py:117
  853.6 15.4 %copy.258 = f32[8,2,2,256,512]{4,0,3,2,1:T(8,128)S(1)} copy(f32[8,2,2,256,512]{4,3,2,1,0:T(8,128)} %all-to-all-done.1) | data formatting | bytes 33554432 | tf_op jit(solution)/shard_map/all_to_all | solution.py:117
  869.0 9.3 fusion.2
  878.3 9.4 fusion.3
  887.7 9.7 fusion.5
  897.4 21.5 %fusion = (f32[2,8,256,512]{3,1,2,0:T(8,128)}, f32[2,8,256,512]{3,1,2,0:T(8,128)}) fusion(f32[8,256]{0,1:T(8,128)S(1)} %copy.152, f32[8,256]{0,1:T(8,128)S(1)} %copy.151, f32[2,256,512,8]{2,3,1,0:T(8,128)} %fusion.2, f32[2,256,512,8]{2,3,1,0:T(8,128)} %fusion.3, f32[2,256,512,8]{2,3,1,0:T(8,128)} %fusion.5, f32[2,2,8,256,512]{4,2,3,1,0:T(8,128)} %bitcast.294), kind=kOutput, calls=%fused_computation.25 | convolution fusion | flops 218104704 | bytes 50348032 | tf_op jit(solution)/shard_map/ka,fabm->fkbm/dot_general | solution.py:10
  918.9 26.4 %fusion.8 = f32[2,8,512,512]{2,3,1,0:T(8,128)} fusion(f32[2,8,256,512]{3,1,2,0:T(8,128)} %get-tuple-element.15, s32[256]{0:T(256)S(1)} %iota_add_fusion), kind=kOutput, calls=%fused_computation.35 | convolution fusion | flops 12886736896 | bytes 25166848 | tf_op jit(solution)/shard_map/qb,fkbm->fqkm/dot_general | solution.py:10
  945.2 25.8 %fusion.6 = f32[2,8,512,512]{2,3,1,0:T(8,128)S(1)} fusion(f32[2,8,256,512]{3,1,2,0:T(8,128)} %get-tuple-element.15, s32[256]{0:T(256)S(1)} %iota_add_fusion), kind=kOutput, calls=%fused_computation.33 | convolution fusion | flops 12886736896 | bytes 25166848 | tf_op jit(solution)/shard_map/qb,fkbm->fqkm/dot_general | solution.py:10
  971.1 49.7 %add_bitcast_fusion = f32[2,512,8,512]{3,1,2,0:T(8,128)} fusion(f32[2,8,512,512]{2,3,1,0:T(8,128)} %fusion.8, f32[2,8,256,512]{3,1,2,0:T(8,128)} %get-tuple-element.14, s32[256]{0:T(256)S(1)} %iota_add_fusion), kind=kOutput, calls=%fused_computation.15 | convolution fusion | flops 12890931200 | bytes 41944064 | tf_op jit(solution)/shard_map/qb,fkbm->fqkm/dot_general | solution.py:10
  1020.8 17.7 %copy.257 = f32[2,512,8,512]{3,2,1,0:T(8,128)} copy(f32[2,512,8,512]{3,1,2,0:T(8,128)} %add_bitcast_fusion) | data formatting | bytes 33554432 | tf_op jit(solution)/shard_map/add | solution.py:67
  1038.5 27.7 %subtract_bitcast_fusion = f32[2,512,8,512]{3,1,2,0:T(8,128)} fusion(f32[2,8,512,512]{2,3,1,0:T(8,128)S(1)} %fusion.6, f32[2,8,256,512]{3,1,2,0:T(8,128)} %get-tuple-element.14, s32[256]{0:T(256)S(1)} %iota_add_fusion), kind=kOutput, calls=%fused_computation.14 | convolution fusion | flops 12890931200 | bytes 41944064 | tf_op jit(solution)/shard_map/qb,fkbm->fqkm/dot_general | solution.py:10
  1066.3 19.3 %copy.256 = f32[2,512,8,512]{3,2,1,0:T(8,128)} copy(f32[2,512,8,512]{3,1,2,0:T(8,128)} %subtract_bitcast_fusion) | data formatting | bytes 33554432 | tf_op jit(solution)/shard_map/sub | solution.py:70
  1085.6 27.6 %multiply_reduce_fusion.3 = (f32[2,512,2]{1,0,2:T(2,128)S(1)}, f32[2,512,2]{1,0,2:T(2,128)S(1)}, f32[2,512,2]{1,0,2:T(2,128)S(1)}, f32[2,512,2]{1,0,2:T(2,128)S(1)}) fusion(f32[2,512,4096]{1,2,0:T(8,128)} %copy.204, f32[1,2,4096,512]{3,2,1,0:T(8,128)} %bitcast.297, f32[1,2,4096,512]{3,2,1,0:T(8,128)S(1)} %bitcast.296, f32[2,512,4096]{1,2,0:T(8,128)} %copy.205, ...), kind=kLoop, calls=%fused_computation.5 | loop fusion | flops 75489280 | bytes 100696064 | tf_op jit(solution)/shard_map/fk,ks,xfks->fxs/dot_general | solution.py:86
  (121 shorter events, 140.2 us)
Async XLA Ops:
  104.0 8.7 copy-start.10
  124.7 10.2 copy-start.8
  124.7 10.2 copy-start.14
  146.8 8.6 copy-start.9
  165.9 60.5 %copy-start.6 = (f32[256,8,512]{2,1,0:T(8,128)}, f32[256,8,512]{2,1,0:T(8,128)S(1)}, u32[]{:S(2)}) copy-start(f32[256,8,512]{2,1,0:T(8,128)S(1)} %get-tuple-element.25) | copy-start | bytes 12582916
  194.6 31.8 %copy-start.19 = (s32[4096]{0:T(1024)S(1)}, s32[4096]{0:T(1024)}, u32[]{:S(2)}) copy-start(s32[4096]{0:T(1024)} %param.10) | copy-start | bytes 49156
  247.8 9.5 copy-start.4
  247.8 9.5 copy-start.13
  278.6 9.5 copy-start.7
  278.6 9.5 copy-start.12
  309.6 9.5 copy-start.5
  309.6 9.5 copy-start.11
  340.4 7.9 copy-start.15
  340.4 7.9 copy-start.16
  348.3 7.7 copy-start.17
  482.9 370.7 %all-to-all-start.1 = ((f32[8,2,2,256,512]{4,3,2,1,0:T(8,128)}), f32[8,2,2,256,512]{4,3,2,1,0:T(8,128)}, u32[]{:S(2)}, u32[]{:S(2)}) async-start(f32[8,2,2,256,512]{4,3,2,1,0:T(8,128)} %copy.149), calls=%async_computation.1 | async-start | bytes 33554432 | tf_op jit(solution)/shard_map/all_to_all | solution.py:117
  490.2 40.1 %all-gather.2.cloned.1.call-start = ((), (), s32[]{:S(2)}) async-start(), calls=%async_computation.3 | async-start | bytes 25165824 | tf_op jit(solution)/shard_map/all_gather | solution.py:135
  498.6 0.8 copy-start.20
  498.6 2.6 copy-start.21
  498.6 14.1 %copy-start.27 = (f32[4]{0:T(128)S(1)}, f32[4]{0:T(128)}, u32[]{:S(2)}) copy-start(f32[4]{0:T(128)} %param.11) | copy-start | bytes 52
  498.6 626.3 %reduce-scatter.4.cloned.1.call-start = ((), (), s32[]{:S(2)}) async-start(), calls=%async_computation.4 | async-start | bytes 393216
  566.2 16.5 %copy-start.1 = (f32[2,512,4096]{1,0,2:T(2,128)S(1)}, f32[2,512,4096]{1,0,2:T(2,128)}, u32[]{:S(2)}) copy-start(f32[2,512,4096]{1,0,2:T(2,128)} %get-tuple-element.47) | copy-start | bytes 50331652
  582.7 8.9 copy-start.18
  611.7 16.5 %copy-start.2 = (f32[2,512,4096]{1,0,2:T(2,128)S(1)}, f32[2,512,4096]{1,0,2:T(2,128)}, u32[]{:S(2)}) copy-start(f32[2,512,4096]{1,0,2:T(2,128)} %get-tuple-element.49) | copy-start | bytes 50331652
  869.0 18.7 %copy-start = (f32[8,2,2,256,512]{4,0,3,2,1:T(8,128)}, f32[8,2,2,256,512]{4,0,3,2,1:T(8,128)S(1)}, u32[]{:S(2)}) copy-start(f32[8,2,2,256,512]{4,0,3,2,1:T(8,128)S(1)} %copy.258) | copy-start | bytes 50331652
  1066.3 19.4 %copy-start.3 = (f32[2,512,8,512]{3,2,1,0:T(8,128)S(1)}, f32[2,512,8,512]{3,2,1,0:T(8,128)}, u32[]{:S(2)}) copy-start(f32[2,512,8,512]{3,2,1,0:T(8,128)} %copy.257) | copy-start | bytes 50331652
  1113.2 18.7 %copy-start.22 = (s32[4]{0:T(128)S(1)}, s32[4]{0:T(128)}, u32[]{:S(2)}) copy-start(s32[4]{0:T(128)} %param.9) | copy-start | bytes 52
  1113.2 18.7 %copy-start.23 = (f32[256]{0:T(256)S(1)}, f32[256]{0:T(256)}, u32[]{:S(2)}) copy-start(f32[256]{0:T(256)} %get-tuple-element.12) | copy-start | bytes 3076
  1113.2 18.7 %copy-start.24 = (f32[256]{0:T(256)S(1)}, f32[256]{0:T(256)}, u32[]{:S(2)}) copy-start(f32[256]{0:T(256)} %compare_select_fusion.7) | copy-start | bytes 3076
  1113.2 18.7 %copy-start.25 = (f32[4]{0:T(128)S(1)}, f32[4]{0:T(128)}, u32[]{:S(2)}) copy-start(f32[4]{0:T(128)} %get-tuple-element.41) | copy-start | bytes 52
  1113.3 18.7 %copy-start.26 = (f32[4]{0:T(128)S(1)}, f32[4]{0:T(128)}, u32[]{:S(2)}) copy-start(f32[4]{0:T(128)} %get-tuple-element.42) | copy-start | bytes 52
Sparse Core Ops, SparseCore 0:
  498.8 31.4 all-gather.1
  1118.2 6.7 reduce-scatter.3
